TPU v7x, 32 devices: a whole 2x2x4 slice. The times are simulated.
32 devices in a mesh: mat: 4 (over z), tile: 8 (over y, x, core).
Axes of the slice: x: 2, y: 2, z: 4, core: 2. Of those that a mesh axis runs over, the one named last changes fastest.
Arguments:
- volume: bfloat16 [4, 64, 8, 1024], P('mat', None, 'tile'), may hold values from -4 to 4
- system: bfloat16 [8, 1024, 32, 128], P('tile'), may hold values from 0 to 0.026977539
- geometry: int32 [8, 16], replicated, may hold values from 0 to 2
- attenuation: float32 [4, 64], replicated, may hold values from 0.05 to 0.5
- response: float32 [8, 64], replicated, may hold values from 0.002 to 0.06
- crosstalk: float32 [8], replicated, may hold values from 0.04 to 0.24
Outputs:
- counts: float32 [8, 64, 16, 512], P(None, ('mat', 'tile'))
Inputs may be any that keep to these rules, and one draw needn't show every extreme that they name: A tile touches, in view v, exactly the 2 detector blocks geometry[t, v] to geometry[t, v] + 1.
All inputs are finite; a program needn't handle non-finite values.
Results may differ from a plain program's by a relative error of at most 0.0003.
Values may be sent and summed in bfloat16 or wider, within the bound.
A program may use at most 128 MiB of HBM per device.

v0:
```python
import jax
import jax.numpy as jnp
from jax import lax
from jax.sharding import PartitionSpec as P

PIXELS = 512
PB = 128
TOUCH = 2
CBINS = 8
SL_DEV = 2
PBLK = 4
KT = 32


def padded_2(x, sides, width):
    for axis, dim in sides:
        devices, length = (lax.axis_size(axis), x.shape[dim])
        up = [(i, (i + 1) % devices) for i in range(devices - 1)]
        down = [(j, i) for i, j in up]
        last = lax.slice_in_dim(x, length - width, length, axis=dim)
        first = lax.slice_in_dim(x, 0, width, axis=dim)
        before = lax.ppermute(last, axis, up)
        after = lax.ppermute(first, axis, down)
        x = jnp.concatenate([before, x, after], axis=dim)
    return x


def place_table(first_block, touch_count, block_count):
    touch_ids = jnp.arange(touch_count, dtype=jnp.int32)
    block_ids = jnp.arange(block_count, dtype=jnp.int32)
    return (first_block[..., None, None] + touch_ids[:, None] == block_ids).astype(jnp.float32)


def per_device(volume, system, geometry, attenuation, response, crosstalk):
    mat_count = lax.axis_size("mat")
    tile_count = lax.axis_size("tile")
    slice_count = volume.shape[1]
    tile_vox = volume.shape[3]
    view_count = geometry.shape[1]
    ray_count = view_count * PIXELS
    matrix = system.reshape(tile_vox, KT * PB)
    columns = volume.reshape(mat_count, tile_count, SL_DEV, tile_vox)
    columns = columns.transpose(1, 0, 2, 3).reshape(slice_count, tile_vox)
    row_share = mat_count * SL_DEV
    partial_value = jnp.dot(columns, matrix, preferred_element_type=jnp.float32)
    partial_value = partial_value.reshape(tile_count, row_share, view_count, TOUCH, PB)
    received = lax.all_to_all(partial_value, "tile", split_axis=0, concat_axis=0, tiled=True)
    placed_all = place_table(geometry, TOUCH, PBLK)
    summed = jnp.einsum("qrvjp,qvjb->rvbp", received, placed_all, precision=lax.Precision.HIGHEST)
    summed = summed.reshape(row_share, ray_count)
    integrals = lax.all_to_all(
        summed.reshape(mat_count, SL_DEV, ray_count), "mat", split_axis=0, concat_axis=0, tiled=True
    )
    stacked = integrals.reshape(mat_count, SL_DEV * ray_count)
    exponent = jnp.dot(
        attenuation.T, stacked, preferred_element_type=jnp.float32, precision=lax.Precision.HIGHEST
    )
    detected = jnp.dot(
        response,
        jnp.exp(-exponent),
        preferred_element_type=jnp.float32,
        precision=lax.Precision.HIGHEST,
    )
    detected = detected.reshape(CBINS, SL_DEV, ray_count)
    padded = padded_2(detected, ((("mat", "tile"), 1),), 1)
    leakage = crosstalk[:, None, None]
    counts = (1.0 - 2.0 * leakage) * detected + leakage * (padded[:, :-2] + padded[:, 2:])
    return counts.reshape(CBINS, SL_DEV, view_count, PIXELS)


def solution(mesh):
    in_specs = (P("mat", None, "tile", None), P("tile", None, None, None), P(), P(), P(), P())
    out_specs = P(None, ("mat", "tile"), None, None)
    return jax.shard_map(
        per_device, mesh=mesh, in_specs=in_specs, out_specs=out_specs, check_vma=False
    )
```

profile of v0, /device:TPU:1, one launch (start us, length us, event | category | flops | bytes accessed | tf_op | source)
XLA Modules:
  0.0 87.6 jit_solution(10779405739836971920)
XLA Ops:
  0.0 0.0 copy-start
  0.0 15.1 %copy.37 = bf16[128,8,32,128]{3,1,2,0:T(8,128)(2,1)} copy(bf16[128,8,32,128]{3,2,1,0:T(8,128)(2,1)} %bitcast.51) | data formatting | bytes 16777216
  15.1 0.0 copy-start.1
  15.1 12.0 %copy.19 = bf16[4096,1024]{1,0:T(8,128)(2,1)} copy(bf16[4096,1024]{0,1:T(8,128)(2,1)} %bitcast.50) | data formatting | bytes 16777216 | tf_op jit(solution)/shard_map/dot_general | solution.py:45
  27.1 0.0 copy-done.1
  27.1 0.1 reshape.32
  27.2 6.0 %fusion.9 = f32[8,8,16,2,128]{4,0,3,2,1:T(8,128)S(1)} fusion(bf16[8,8,1024,1,1]{2,0,4,3,1:T(8,128)(2,1)S(1)} %bitcast.60, bf16[16,2,128,1024,1]{3,2,1,0,4:T(8,128)(2,1)} %bitcast.52), kind=kOutput, calls=%fused_computation.17 | convolution fusion | flops 536870912 | bytes 9568256 | tf_op jit(solution)/shard_map/dot_general | solution.py:45
  33.2 0.0 copy-start.2
  33.2 0.0 copy-start.3
  33.2 1.5 %copy.20 = f32[8,8,16,2,128]{4,3,1,2,0:T(2,128)} copy(f32[8,8,16,2,128]{4,0,3,2,1:T(8,128)S(1)} %fusion.9) | data formatting | bytes 2097152 | tf_op jit(solution)/shard_map/dot_general | solution.py:45
  34.7 5.2 %all-to-all-start = ((f32[8,8,16,2,128]{4,3,1,2,0:T(2,128)}), f32[8,8,16,2,128]{4,3,1,2,0:T(2,128)S(1)}, u32[]{:S(2)}, u32[]{:S(2)}) async-start(f32[8,8,16,2,128]{4,3,1,2,0:T(2,128)} %copy.20), calls=%async_computation | async-start | bytes 2097152 | tf_op jit(solution)/shard_map/all_to_all | solution.py:47
  40.0 0.0 copy-done.2
  40.0 0.1 copy.17
  40.0 11.9 %all-to-all-done = f32[8,8,16,2,128]{4,3,1,2,0:T(2,128)S(1)} async-done(((f32[8,8,16,2,128]{4,3,1,2,0:T(2,128)}), f32[8,8,16,2,128]{4,3,1,2,0:T(2,128)S(1)}, u32[]{:S(2)}, u32[]{:S(2)}) %all-to-all-start) | async-done | bytes 1048608 | tf_op jit(solution)/shard_map/all_to_all | solution.py:47
  51.9 1.1 %convolution_bitcast_fusion = f32[8,16,4,128]{3,2,0,1:T(4,128)S(1)} fusion(f32[8,8,16,2,128]{4,3,1,2,0:T(2,128)S(1)} %all-to-all-done, s32[8,16,2]{0,2,1:T(2,128)S(1)} %iota_add_fusion), kind=kOutput, calls=%fused_computation.3 | convolution fusion | flops 12583936 | bytes 1311744 | tf_op jit(solution)/shard_map/qrvjp,qvjb->rvbp/dot_general | solution.py:49
  53.0 0.2 reshape_reshape.3
  53.3 10.4 %all_to_all.10 = f32[4,2,8192]{2,1,0:T(2,128)S(1)} all-to-all(f32[4,2,8192]{2,1,0:T(2,128)S(1)} %reshape_reshape.3), channel_id=1, replica_groups=mesh['mat'=4,'tile'=8] {'mat'}, dimensions={0} | all-to-all | bytes 524288 | tf_op jit(solution)/shard_map/all_to_all | solution.py:51
  63.6 0.2 copy.31
  63.8 0.0 copy-done.3
  63.8 0.0 copy-start.4
  63.8 3.6 %fusion = f32[16384,64]{0,1:T(8,128)S(1)} fusion(f32[4,16384]{1,0:T(4,128)S(1)} %bitcast.57, f32[4,64]{1,0:T(4,128)S(1)} %copy-done.3), kind=kOutput, calls=%fused_computation.1 | convolution fusion | flops 51380224 | bytes 4457472 | tf_op jit(solution)/shard_map/dot_general | solution.py:55
  67.4 0.0 copy-done
  67.4 2.3 %fusion.10 = f32[16384,8]{0,1:T(8,128)S(1)} fusion(f32[16384,64]{0,1:T(8,128)S(1)} %fusion, f32[8,64]{1,0:T(8,128)S(1)} %copy-done), kind=kOutput, calls=%fused_computation.18 | convolution fusion | flops 100663296 | bytes 4720640 | tf_op jit(solution)/shard_map/dot_general | solution.py:58
  69.7 8.9 %collective-permute-start = (f32[8,1,8192]{2,0,1:T(8,128)S(1)}, f32[8,1,8192]{2,0,1:T(8,128)S(1)}, u32[]{:S(2)}, u32[]{:S(2)}) collective-permute-start(f32[8,1,8192]{2,0,1:T(8,128)S(1)} %get-tuple-element.5), channel_id=1, source_target_pairs={{0,1},{1,2},{2,3},{3,4},{4,5},{5,6},{6,7},{7,8},{8,9},{9,10},{10,1... | collective-permute-start | bytes 786440 | tf_op jit(solution)/shard_map/ppermute | solution.py:22
  78.6 1.9 %collective-permute-start.1 = (f32[8,1,8192]{2,0,1:T(8,128)S(1)}, f32[8,1,8192]{2,0,1:T(8,128)S(1)}, u32[]{:S(2)}, u32[]{:S(2)}) collective-permute-start(f32[8,1,8192]{2,0,1:T(8,128)S(1)} %get-tuple-element.6), channel_id=1, source_target_pairs={{1,0},{2,1},{3,2},{4,3},{5,4},{6,5},{7,6},{8,7},{9,8},{10,9},{11,1... | collective-permute-start | bytes 786440 | tf_op jit(solution)/shard_map/ppermute | solution.py:23
  80.5 0.0 copy-done.4
  80.5 1.3 %collective-permute-done = f32[8,1,8192]{2,0,1:T(8,128)S(1)} collective-permute-done((f32[8,1,8192]{2,0,1:T(8,128)S(1)}, f32[8,1,8192]{2,0,1:T(8,128)S(1)}, u32[]{:S(2)}, u32[]{:S(2)}) %collective-permute-start) | collective-permute-done | bytes 262176 | tf_op jit(solution)/shard_map/ppermute | solution.py:22
  81.8 4.4 %collective-permute-done.1 = f32[8,1,8192]{2,0,1:T(8,128)S(1)} collective-permute-done((f32[8,1,8192]{2,0,1:T(8,128)S(1)}, f32[8,1,8192]{2,0,1:T(8,128)S(1)}, u32[]{:S(2)}, u32[]{:S(2)}) %collective-permute-start.1) | collective-permute-done | bytes 262176 | tf_op jit(solution)/shard_map/ppermute | solution.py:23
  86.2 0.2 fusion.4
  86.4 0.3 copy.38
  86.7 0.8 copy.29
  (5 shorter events, 0.1 us)
Async XLA Ops:
  0.0 67.4 %copy-start = (f32[8,64]{1,0:T(8,128)S(1)}, f32[8,64]{1,0:T(8,128)}, u32[]{:S(2)}) copy-start(f32[8,64]{1,0:T(8,128)} %param.10) | copy-start | bytes 6148
  15.1 12.0 %copy-start.1 = (bf16[1,64,1,1024]{3,1,2,0:T(8,128)(2,1)S(1)}, bf16[1,64,1,1024]{3,1,2,0:T(8,128)(2,1)}, u32[]{:S(2)}) copy-start(bf16[1,64,1,1024]{3,1,2,0:T(8,128)(2,1)} %param.6) | copy-start | bytes 393220
  33.2 6.7 %copy-start.2 = (s32[8,16]{1,0:T(8,128)S(1)}, s32[8,16]{1,0:T(8,128)}, u32[]{:S(2)}) copy-start(s32[8,16]{1,0:T(8,128)} %param.8) | copy-start | bytes 1540
  33.2 30.6 %copy-start.3 = (f32[4,64]{1,0:T(4,128)S(1)}, f32[4,64]{1,0:T(4,128)}, u32[]{:S(2)}) copy-start(f32[4,64]{1,0:T(4,128)} %param.9) | copy-start | bytes 3076
  34.7 17.2 %all-to-all-start = ((f32[8,8,16,2,128]{4,3,1,2,0:T(2,128)}), f32[8,8,16,2,128]{4,3,1,2,0:T(2,128)S(1)}, u32[]{:S(2)}, u32[]{:S(2)}) async-start(f32[8,8,16,2,128]{4,3,1,2,0:T(2,128)} %copy.20), calls=%async_computation | async-start | bytes 2097152 | tf_op jit(solution)/shard_map/all_to_all | solution.py:47
  63.8 16.7 %copy-start.4 = (f32[8]{0:T(128)S(1)}, f32[8]{0:T(128)}, u32[]{:S(2)}) copy-start(f32[8]{0:T(128)} %param.11) | copy-start | bytes 100
  69.7 12.2 %collective-permute-start = (f32[8,1,8192]{2,0,1:T(8,128)S(1)}, f32[8,1,8192]{2,0,1:T(8,128)S(1)}, u32[]{:S(2)}, u32[]{:S(2)}) collective-permute-start(f32[8,1,8192]{2,0,1:T(8,128)S(1)} %get-tuple-element.5), channel_id=1, source_target_pairs={{0,1},{1,2},{2,3},{3,4},{4,5},{5,6},{6,7},{7,8},{8,9},{9,10},{10,1... | collective-permute-start | bytes 786440 | tf_op jit(solution)/shard_map/ppermute | solution.py:22
  78.6 7.7 %collective-permute-start.1 = (f32[8,1,8192]{2,0,1:T(8,128)S(1)}, f32[8,1,8192]{2,0,1:T(8,128)S(1)}, u32[]{:S(2)}, u32[]{:S(2)}) collective-permute-start(f32[8,1,8192]{2,0,1:T(8,128)S(1)} %get-tuple-element.6), channel_id=1, source_target_pairs={{1,0},{2,1},{3,2},{4,3},{5,4},{6,5},{7,6},{8,7},{9,8},{10,9},{11,1... | collective-permute-start | bytes 786440 | tf_op jit(solution)/shard_map/ppermute | solution.py:23
where the time goes:
time: 88.1 us; the launch traced here: 87.6 us
  local copies, waits for them, and re-layouts  30.4 us (35%)
  waiting for transfers between devices  17.6 us (20%)
  starting transfers between devices  16 us (18%)
  matrix products  12.9 us (15%)
  blocking collectives  10.4 us (12%)
    unnamed x14, local copies, waits for them, and re-layouts  15.7 us
    dot_general x2, local copies, waits for them, and re-layouts, per_device(): partial_value = jnp.dot(columns, matrix, preferred_element_type=jnp.float32)  13.5 us
    all_to_all x1, waiting for transfers between devices, per_device(): lax.all_to_all(partial_value, 'tile', split_axis=0, concat_axis=0, tiled=...  11.9 us
    all_to_all x1, blocking collectives, per_device(): lax.all_to_all(summed.reshape(mat_count, SL_DEV, ray_count), 'mat', split...  10.4 us
    ppermute x1, starting transfers between devices, padded_2(): before = lax.ppermute(last, axis, up)  8.85 us
    dot_general x1, matrix products, per_device(): partial_value = jnp.dot(columns, matrix, preferred_element_type=jnp.float32)  6.04 us
    all_to_all x1, starting transfers between devices, per_device(): lax.all_to_all(partial_value, 'tile', split_axis=0, concat_axis=0, tiled=...  5.21 us
    ppermute x1, waiting for transfers between devices, padded_2(): after = lax.ppermute(first, axis, down)  4.4 us
  transfers between devices with their start and end apart: 3, of which 3 were waited for; matrix products, arithmetic and copies ran while one was open for 0% of the time, Pallas kernels for 0%

commit v1 on v0

v1 whole, which is shorter than its diff:
```python
import functools

import jax
import jax.numpy as jnp
import numpy as np
from jax import lax
from jax.experimental import pallas as pl
from jax.experimental.pallas import tpu as pltpu
from jax.sharding import PartitionSpec as P

PIXELS = 512
GROUPS = 4
LOG2E = 1.4426950408889634
MESH = pl.DeviceIdType.MESH
LINK = jnp.float32


def loop(low, high, body):
    if high - low <= 8:
        for index in range(low, high):
            body(index)
    else:
        lax.fori_loop(low, high, lambda index, _: (body(index), 0)[1], 0)


def kernel(mats, tiles, slices, voxels, views, touch, pb, pblk, ebins, cbins,
           order_ref, volume_ref, system_ref, geometry_ref, attenuation_ref, response_ref, crosstalk_ref,
           counts_ref,
           matrix, permuted, partial_out, partial_in, summed_out, summed_in, detected, before, after,
           matrix_sem, send1, recv1, send2, recv2, send3, recv3):
    me_mat, me_tile = lax.axis_index("mat"), lax.axis_index("tile")
    devices = mats * tiles
    me = me_mat * tiles + me_tile
    rows = slices // devices
    share = mats * rows
    group_views = views // GROUPS
    group_cols = group_views * touch
    rays = group_views * pblk
    has_prev, has_next = me > 0, me < devices - 1
    up, down = me + 1, me - 1

    loads = [
        pltpu.make_async_copy(system_ref.at[:, pl.ds(g * group_cols, group_cols)], matrix.at[g], matrix_sem.at[g])
        for g in range(GROUPS)
    ]
    for load in loads:
        load.start()

    barrier = pltpu.get_barrier_semaphore()

    def greet_tile(off):
        pl.semaphore_signal(barrier, inc=1, device_id={"tile": lax.rem(me_tile + off, tiles)}, device_id_type=MESH)

    def greet_mat(off):
        pl.semaphore_signal(barrier, inc=1, device_id={"mat": lax.rem(me_mat + off, mats)}, device_id_type=MESH)

    def place(device):
        return {"mat": device // tiles, "tile": lax.rem(device, tiles)}

    loop(1, tiles, greet_tile)
    loop(1, mats, greet_mat)

    @pl.when(has_prev)
    def _():
        pl.semaphore_signal(barrier, inc=1, device_id=place(down), device_id_type=MESH)

    @pl.when(has_next)
    def _():
        pl.semaphore_signal(barrier, inc=1, device_id=place(up), device_id_type=MESH)

    permuted[...] = jnp.dot(order_ref[...], volume_ref[...], preferred_element_type=jnp.float32).astype(jnp.bfloat16)

    def copy1(g, off):
        peer = lax.rem(me_tile + off, tiles)
        return pltpu.make_async_remote_copy(
            src_ref=partial_out.at[g, peer], dst_ref=partial_in.at[g, me_tile],
            send_sem=send1.at[g, peer], recv_sem=recv1.at[g, me_tile],
            device_id={"tile": peer}, device_id_type=MESH)

    def arrival1(g, off):
        peer = lax.rem(me_tile + off, tiles)
        return pltpu.make_async_remote_copy(
            src_ref=partial_out.at[g, peer], dst_ref=partial_in.at[g, peer],
            send_sem=send1.at[g, peer], recv_sem=recv1.at[g, peer],
            device_id={"tile": peer}, device_id_type=MESH)

    def copy2(g, off):
        peer = lax.rem(me_mat + off, mats)
        return pltpu.make_async_remote_copy(
            src_ref=summed_out.at[g, peer], dst_ref=summed_in.at[g, me_mat],
            send_sem=send2.at[g, peer], recv_sem=recv2.at[g, me_mat],
            device_id={"mat": peer}, device_id_type=MESH)

    def arrival2(g, off):
        peer = lax.rem(me_mat + off, mats)
        return pltpu.make_async_remote_copy(
            src_ref=summed_out.at[g, peer], dst_ref=summed_in.at[g, peer],
            send_sem=send2.at[g, peer], recv_sem=recv2.at[g, peer],
            device_id={"mat": peer}, device_id_type=MESH)

    def copy_down(g):
        return pltpu.make_async_remote_copy(
            src_ref=detected.at[g, 0], dst_ref=after.at[g],
            send_sem=send3.at[g, 0], recv_sem=recv3.at[g, 0],
            device_id=place(down), device_id_type=MESH)

    def copy_up(g):
        return pltpu.make_async_remote_copy(
            src_ref=detected.at[g, rows - 1], dst_ref=before.at[g],
            send_sem=send3.at[g, 1], recv_sem=recv3.at[g, 1],
            device_id=place(up), device_id_type=MESH)

    def multiply(g):
        loads[g].wait()
        columns = jnp.swapaxes(matrix[g], 0, 1)
        for k in range(0, group_cols, 2):
            pair = jnp.concatenate([columns[k], columns[k + 1]], axis=-1)
            product = jnp.dot(permuted[...], pair, preferred_element_type=jnp.float32)
            product = product.reshape(tiles, share, 2 * pb)
            partial_out[g, :, k] = product[:, :, :pb].astype(LINK)
            partial_out[g, :, k + 1] = product[:, :, pb:].astype(LINK)
        if g == 0:
            pl.semaphore_wait(
                barrier, tiles - 1 + mats - 1 + has_prev.astype(jnp.int32) + has_next.astype(jnp.int32))
        loop(1, tiles, lambda off: copy1(g, off).start())
        partial_in[g, me_tile] = partial_out[g, me_tile]

    def add_tiles(g):
        loop(1, tiles, lambda off: arrival1(g, off).wait_recv())

        def add(tile, sums):
            sums = list(sums)
            for v in range(group_views):
                first = geometry_ref[tile, g * group_views + v]
                for j in range(touch):
                    value = partial_in[g, tile, v * touch + j].astype(jnp.float32)
                    for b in range(j, pblk - touch + 1 + j):
                        weight = (first + j == b).astype(jnp.float32)
                        sums[b * group_views + v] += weight * value
            return tuple(sums)

        sums = tuple(jnp.zeros((share, pb), jnp.float32) for _ in range(rays))
        if tiles <= 8:
            for tile in range(tiles):
                sums = add(tile, sums)
        else:
            sums = lax.fori_loop(0, tiles, add, sums)
        by_row = jnp.swapaxes(jnp.stack(sums, axis=0), 0, 1)
        summed_out[g] = by_row.reshape(mats, rows, rays, pb).astype(LINK)
        loop(1, mats, lambda off: copy2(g, off).start())
        summed_in[g, me_mat] = summed_out[g, me_mat]

    def detect(g):
        loop(1, mats, lambda off: arrival2(g, off).wait_recv())
        scaled = [summed_in[g, m].astype(jnp.float32).reshape(rows * rays, pb) * (-LOG2E) for m in range(mats)]
        unroll = 8

        def energies(block, totals):
            totals = list(totals)
            for inner in range(unroll):
                e = block * unroll + inner
                power = attenuation_ref[0, e] * scaled[0]
                for m in range(1, mats):
                    power += attenuation_ref[m, e] * scaled[m]
                passed = jnp.exp2(power)
                for b in range(cbins):
                    totals[b] += response_ref[b, e] * passed
            return tuple(totals)

        totals = tuple(jnp.zeros((rows * rays, pb), jnp.float32) for _ in range(cbins))
        totals = lax.fori_loop(0, ebins // unroll, energies, totals)
        for b in range(cbins):
            for r in range(rows):
                detected[g, r, b] = totals[b][r * rays:(r + 1) * rays]

        @pl.when(has_prev)
        def _():
            copy_down(g).start()

        @pl.when(has_next)
        def _():
            copy_up(g).start()

    def count(g):
        @pl.when(has_prev)
        def _():
            copy_up(g).wait_recv()

        @pl.when(has_next)
        def _():
            copy_down(g).wait_recv()

        for b in range(cbins):
            leak = crosstalk_ref[b]
            keep = 1.0 - 2.0 * leak
            for r in range(rows):
                lower = detected[g, r - 1, b] if r > 0 else before[g, b]
                upper = detected[g, r + 1, b] if r < rows - 1 else after[g, b]
                value = keep * detected[g, r, b] + leak * (lower + upper)
                for k in range(pblk):
                    counts_ref[b, r, g * group_views:(g + 1) * group_views, k * pb:(k + 1) * pb] = (
                        value[k * group_views:(k + 1) * group_views])

    @pl.when(jnp.logical_not(has_prev))
    def _():
        before[...] = jnp.zeros_like(before)

    @pl.when(jnp.logical_not(has_next))
    def _():
        after[...] = jnp.zeros_like(after)

    multiply(0)
    multiply(1)
    multiply(2)
    add_tiles(0)
    multiply(3)
    add_tiles(1)
    detect(0)
    add_tiles(2)
    detect(1)
    add_tiles(3)
    detect(2)
    detect(3)
    for g in range(GROUPS):
        count(g)
    for g in range(GROUPS):
        loop(1, tiles, lambda off: copy1(g, off).wait_send())
        loop(1, mats, lambda off: copy2(g, off).wait_send())

        @pl.when(has_prev)
        def _():
            copy_down(g).wait_send()

        @pl.when(has_next)
        def _():
            copy_up(g).wait_send()


def per_device(mats, tiles, volume, system, geometry, attenuation, response, crosstalk):
    slices, voxels = volume.shape[1], volume.shape[3]
    views = geometry.shape[1]
    columns, pb = system.shape[2], system.shape[3]
    touch = columns // views
    pblk = PIXELS // pb
    ebins, cbins = attenuation.shape[1], response.shape[0]
    rows = slices // (mats * tiles)
    share = mats * rows
    group_views = views // GROUPS
    rays = group_views * pblk
    source = np.arange(slices).reshape(mats, tiles, rows).transpose(1, 0, 2).reshape(-1)
    order = jnp.asarray(np.eye(slices, dtype=np.float32)[source], jnp.bfloat16)
    vmem = pl.BlockSpec(memory_space=pltpu.VMEM)
    smem = pl.BlockSpec(memory_space=pltpu.SMEM)
    dma = pltpu.SemaphoreType.DMA
    return pl.pallas_call(
        functools.partial(kernel, mats, tiles, slices, voxels, views, touch, pb, pblk, ebins, cbins),
        out_shape=jax.ShapeDtypeStruct((cbins, rows, views, PIXELS), jnp.float32),
        in_specs=[vmem, vmem, pl.BlockSpec(memory_space=pl.ANY), smem, smem, smem, smem],
        out_specs=vmem,
        scratch_shapes=[
            pltpu.VMEM((GROUPS, voxels, columns // GROUPS, pb), jnp.bfloat16),
            pltpu.VMEM((slices, voxels), jnp.bfloat16),
            pltpu.VMEM((GROUPS, tiles, columns // GROUPS, share, pb), LINK),
            pltpu.VMEM((GROUPS, tiles, columns // GROUPS, share, pb), LINK),
            pltpu.VMEM((GROUPS, mats, rows, rays, pb), LINK),
            pltpu.VMEM((GROUPS, mats, rows, rays, pb), LINK),
            pltpu.VMEM((GROUPS, rows, cbins, rays, pb), jnp.float32),
            pltpu.VMEM((GROUPS, cbins, rays, pb), jnp.float32),
            pltpu.VMEM((GROUPS, cbins, rays, pb), jnp.float32),
            dma((GROUPS,)),
            dma((GROUPS, tiles)),
            dma((GROUPS, tiles)),
            dma((GROUPS, mats)),
            dma((GROUPS, mats)),
            dma((GROUPS, 2)),
            dma((GROUPS, 2)),
        ],
        compiler_params=pltpu.CompilerParams(
            collective_id=0, has_side_effects=True, vmem_limit_bytes=60 * 2**20
        ),
        name="project",
    )(order, volume.reshape(slices, voxels), system.reshape(voxels, columns, pb), geometry, attenuation,
      response, crosstalk)


def solution(mesh):
    in_specs = (P("mat", None, "tile", None), P("tile", None, None, None), P(), P(), P(), P())
    out_specs = P(None, ("mat", "tile"), None, None)
    body = functools.partial(per_device, mesh.shape["mat"], mesh.shape["tile"])
    return jax.shard_map(body, mesh=mesh, in_specs=in_specs, out_specs=out_specs, check_vma=False)
```

time: 88.1 us -> 32 us (0.36)
  Pallas kernels: 0 us -> 30 us
  local copies, waits for them, and re-layouts: 30.4 us -> 1.88 us
  waiting for transfers between devices: 17.6 us -> 0 us
  starting transfers between devices: 16 us -> 0 us
  matrix products: 12.9 us -> 0 us
  blocking collectives: 10.4 us -> 0 us
    pallas_call x0 -> x1, Pallas kernels: none -> 30 us  [per_device(): pl.pallas_call(functools.partial(kernel, mats, tiles, slices, voxels, vie...]
    unnamed x14 -> x1, local copies, waits for them, and re-layouts: 15.7 us -> 1.88 us
    dot_general x2 -> x0, local copies, waits for them, and re-layouts: 13.5 us -> none  [per_device(): partial_value = jnp.dot(columns, matrix, preferred_element_type=jnp.float32)]
    dot_general x4 -> x0, matrix products: 12.9 us -> none  [the longest x1 6.04 us: per_device(): partial_value = jnp.dot(columns, matrix, preferred_element_type=jnp.float32)]
    all_to_all x1 -> x0, waiting for transfers between devices: 11.9 us -> none  [per_device(): lax.all_to_all(partial_value, 'tile', split_axis=0, concat_axis=0, tiled=...]
    ppermute x2 -> x0, starting transfers between devices: 10.8 us -> none  [the longest x1 8.85 us: padded_2(): before = lax.ppermute(last, axis, up)]
    all_to_all x1 -> x0, blocking collectives: 10.4 us -> none  [per_device(): lax.all_to_all(summed.reshape(mat_count, SL_DEV, ray_count), 'mat', split...]
    ppermute x2 -> x0, waiting for transfers between devices: 5.74 us -> none  [the longest x1 4.4 us: padded_2(): after = lax.ppermute(first, axis, down)]
  transfers between devices with their start and end apart: 3 -> 0, of which waited for: 3 -> 0; matrix products, arithmetic and copies ran while one was open for 0% -> 0% of each run, Pallas kernels for 0% -> 0%
where the time goes in v1:
time: 32 us; the launch traced here: 31.9 us
  Pallas kernels  30 us (94%)
  local copies, waits for them, and re-layouts  1.88 us (6%)
    pallas_call x1, Pallas kernels, per_device(): pl.pallas_call(functools.partial(kernel, mats, tiles, slices, voxels, vie...  30 us
    unnamed x1, local copies, waits for them, and re-layouts  1.88 us

profile of v1, /device:TPU:1, one launch (start us, length us, event | category | flops | bytes accessed | tf_op | source)
XLA Modules:
  0.0 31.9 jit_solution(9361752405137837661)
XLA Ops:
  0.0 30.0 %project.1 = f32[8,2,16,512]{3,2,1,0:T(8,128)} custom-call(bf16[64,64]{1,0:T(8,128)(2,1)} %constant.2.clone.order_ref, bf16[64,1024]{1,0:T(8,128)(2,1)} %bitcast.3, bf16[1024,32,128]{2,1,0:T(8,128)(2,1)} %bitcast.2, s32[8,16]{1,0:T(8,128)} %geometry_ref.1, f32[4,64]{1,0:T(4,128)} %attenuation_ref.1, f32[8,64]{1,0:T(8,128)} %response_ref.1, f32[8]{0:T(128)} %crosstalk_ref.1), custom_call_target="tpu_custom_call" | custom-call | tf_op jit(solution)/shard_map/project/pallas_call | solution.py:255
  30.0 1.9 %copy.9 = f32[8,2,16,512]{3,2,1,0:T(8,128)} copy(f32[8,2,16,512]{3,2,1,0:T(8,128)} %project.1) | data formatting | bytes 1048576

commit v2 on v1

--- a/solution.py
+++ b/solution.py
@@ -2,7 +2,6 @@
 
 import jax
 import jax.numpy as jnp
-import numpy as np
 from jax import lax
 from jax.experimental import pallas as pl
 from jax.experimental.pallas import tpu as pltpu
@@ -10,9 +9,9 @@
 
 PIXELS = 512
 GROUPS = 4
+EARLY = 2
 LOG2E = 1.4426950408889634
 MESH = pl.DeviceIdType.MESH
-LINK = jnp.float32
 
 
 def loop(low, high, body):
@@ -24,15 +23,14 @@
 
 
 def kernel(mats, tiles, slices, voxels, views, touch, pb, pblk, ebins, cbins,
-           order_ref, volume_ref, system_ref, geometry_ref, attenuation_ref, response_ref, crosstalk_ref,
+           volume_ref, system_ref, geometry_ref, attenuation_ref, response_ref, crosstalk_ref,
            counts_ref,
-           matrix, permuted, partial_out, partial_in, summed_out, summed_in, detected, before, after,
-           matrix_sem, send1, recv1, send2, recv2, send3, recv3):
+           matrix, gathered, partial_out, partial_in, summed_out, summed_in, detected, before, after,
+           matrix_sem, send0, recv0, send1, recv1, send2, recv2, send3, recv3):
     me_mat, me_tile = lax.axis_index("mat"), lax.axis_index("tile")
     devices = mats * tiles
     me = me_mat * tiles + me_tile
     rows = slices // devices
-    share = mats * rows
     group_views = views // GROUPS
     group_cols = group_views * touch
     rays = group_views * pblk
@@ -68,7 +66,21 @@
     def _():
         pl.semaphore_signal(barrier, inc=1, device_id=place(up), device_id_type=MESH)
 
-    permuted[...] = jnp.dot(order_ref[...], volume_ref[...], preferred_element_type=jnp.float32).astype(jnp.bfloat16)
+    gathered[me_mat] = volume_ref[me_mat]
+
+    def copy0(off):
+        peer = lax.rem(me_mat + off, mats)
+        return pltpu.make_async_remote_copy(
+            src_ref=volume_ref.at[peer], dst_ref=gathered.at[me_mat],
+            send_sem=send0.at[peer], recv_sem=recv0.at[me_mat],
+            device_id={"mat": peer}, device_id_type=MESH)
+
+    def arrival0(off):
+        peer = lax.rem(me_mat + off, mats)
+        return pltpu.make_async_remote_copy(
+            src_ref=volume_ref.at[peer], dst_ref=gathered.at[peer],
+            send_sem=send0.at[peer], recv_sem=recv0.at[peer],
+            device_id={"mat": peer}, device_id_type=MESH)
 
     def copy1(g, off):
         peer = lax.rem(me_tile + off, tiles)
@@ -113,46 +125,72 @@
     def multiply(g):
         loads[g].wait()
         columns = jnp.swapaxes(matrix[g], 0, 1)
-        for k in range(0, group_cols, 2):
-            pair = jnp.concatenate([columns[k], columns[k + 1]], axis=-1)
-            product = jnp.dot(permuted[...], pair, preferred_element_type=jnp.float32)
-            product = product.reshape(tiles, share, 2 * pb)
-            partial_out[g, :, k] = product[:, :, :pb].astype(LINK)
-            partial_out[g, :, k + 1] = product[:, :, pb:].astype(LINK)
         if g == 0:
             pl.semaphore_wait(
                 barrier, tiles - 1 + mats - 1 + has_prev.astype(jnp.int32) + has_next.astype(jnp.int32))
+            loop(1, mats, lambda off: copy0(off).start())
+        if g == EARLY:
+            loop(1, mats, lambda off: arrival0(off).wait_recv())
+        source = volume_ref if g < EARLY else gathered
+        rows_in = source[...].reshape(slices, voxels)
+        products = [None] * group_cols
+        for k in range(0, group_cols, 2):
+            pair = jnp.concatenate([columns[k], columns[k + 1]], axis=-1)
+            product = jnp.dot(rows_in, pair, preferred_element_type=jnp.float32)
+            for i in range(2):
+                v, j = divmod(k + i, touch)
+                products[j * group_views + v] = product[:, i * pb:(i + 1) * pb]
+        by_row = jnp.swapaxes(jnp.stack(products, axis=0), 0, 1)
+        by_row = by_row.reshape(mats, tiles, rows, group_cols, pb)
+        for m in range(mats):
+            partial_out[g, :, m] = by_row[m]
         loop(1, tiles, lambda off: copy1(g, off).start())
         partial_in[g, me_tile] = partial_out[g, me_tile]
 
     def add_tiles(g):
         loop(1, tiles, lambda off: arrival1(g, off).wait_recv())
 
+        sublane = lax.broadcasted_iota(jnp.int32, (group_cols, pb), 0)
+        view = lax.rem(sublane, group_views)
+        half = sublane < group_views
+
         def add(tile, sums):
             sums = list(sums)
-            for v in range(group_views):
-                first = geometry_ref[tile, g * group_views + v]
-                for j in range(touch):
-                    value = partial_in[g, tile, v * touch + j].astype(jnp.float32)
-                    for b in range(j, pblk - touch + 1 + j):
-                        weight = (first + j == b).astype(jnp.float32)
-                        sums[b * group_views + v] += weight * value
+            first = jnp.full((group_cols, pb), geometry_ref[tile, g * group_views], jnp.int32)
+            for v in range(1, group_views):
+                first = jnp.where(view == v, geometry_ref[tile, g * group_views + v], first)
+            low, middle, high = first == 0, first == 1, first == 2
+            low_turned = jnp.logical_and(middle, jnp.logical_not(half))
+            high_turned = jnp.logical_and(middle, half)
+            for m in range(mats):
+                for r in range(rows):
+                    value = partial_in[g, tile, m, r]
+                    turned = jnp.concatenate([value[group_views:], value[:group_views]], axis=0)
+                    at = 2 * (m * rows + r)
+                    sums[at] += jnp.where(low, value, jnp.where(low_turned, turned, 0.0))
+                    sums[at + 1] += jnp.where(high, value, jnp.where(high_turned, turned, 0.0))
             return tuple(sums)
 
-        sums = tuple(jnp.zeros((share, pb), jnp.float32) for _ in range(rays))
+        sums = tuple(jnp.zeros((group_cols, pb), jnp.float32) for _ in range(2 * mats * rows))
         if tiles <= 8:
             for tile in range(tiles):
                 sums = add(tile, sums)
         else:
             sums = lax.fori_loop(0, tiles, add, sums)
-        by_row = jnp.swapaxes(jnp.stack(sums, axis=0), 0, 1)
-        summed_out[g] = by_row.reshape(mats, rows, rays, pb).astype(LINK)
-        loop(1, mats, lambda off: copy2(g, off).start())
-        summed_in[g, me_mat] = summed_out[g, me_mat]
+        target = summed_out if g < EARLY else summed_in
+        for m in range(mats):
+            for r in range(rows):
+                at = 2 * (m * rows + r)
+                target[g, m, r, :group_cols] = sums[at]
+                target[g, m, r, group_cols:] = sums[at + 1]
+        if g < EARLY:
+            loop(1, mats, lambda off: copy2(g, off).start())
+            summed_in[g, me_mat] = summed_out[g, me_mat]
 
     def detect(g):
-        loop(1, mats, lambda off: arrival2(g, off).wait_recv())
-        scaled = [summed_in[g, m].astype(jnp.float32).reshape(rows * rays, pb) * (-LOG2E) for m in range(mats)]
+        if g < EARLY:
+            loop(1, mats, lambda off: arrival2(g, off).wait_recv())
+        scaled = [summed_in[g, m].reshape(rows * rays, pb) * (-LOG2E) for m in range(mats)]
         unroll = 8
 
         def energies(block, totals):
@@ -223,9 +261,11 @@
     detect(3)
     for g in range(GROUPS):
         count(g)
+    loop(1, mats, lambda off: copy0(off).wait_send())
     for g in range(GROUPS):
         loop(1, tiles, lambda off: copy1(g, off).wait_send())
-        loop(1, mats, lambda off: copy2(g, off).wait_send())
+        if g < EARLY:
+            loop(1, mats, lambda off: copy2(g, off).wait_send())
 
         @pl.when(has_prev)
         def _():
@@ -244,30 +284,30 @@
     pblk = PIXELS // pb
     ebins, cbins = attenuation.shape[1], response.shape[0]
     rows = slices // (mats * tiles)
-    share = mats * rows
     group_views = views // GROUPS
     rays = group_views * pblk
-    source = np.arange(slices).reshape(mats, tiles, rows).transpose(1, 0, 2).reshape(-1)
-    order = jnp.asarray(np.eye(slices, dtype=np.float32)[source], jnp.bfloat16)
+    assert touch == 2 and pblk == 2 * touch
     vmem = pl.BlockSpec(memory_space=pltpu.VMEM)
     smem = pl.BlockSpec(memory_space=pltpu.SMEM)
     dma = pltpu.SemaphoreType.DMA
     return pl.pallas_call(
         functools.partial(kernel, mats, tiles, slices, voxels, views, touch, pb, pblk, ebins, cbins),
         out_shape=jax.ShapeDtypeStruct((cbins, rows, views, PIXELS), jnp.float32),
-        in_specs=[vmem, vmem, pl.BlockSpec(memory_space=pl.ANY), smem, smem, smem, smem],
+        in_specs=[vmem, pl.BlockSpec(memory_space=pl.ANY), smem, smem, smem, smem],
         out_specs=vmem,
         scratch_shapes=[
             pltpu.VMEM((GROUPS, voxels, columns // GROUPS, pb), jnp.bfloat16),
-            pltpu.VMEM((slices, voxels), jnp.bfloat16),
-            pltpu.VMEM((GROUPS, tiles, columns // GROUPS, share, pb), LINK),
-            pltpu.VMEM((GROUPS, tiles, columns // GROUPS, share, pb), LINK),
-            pltpu.VMEM((GROUPS, mats, rows, rays, pb), LINK),
-            pltpu.VMEM((GROUPS, mats, rows, rays, pb), LINK),
+            pltpu.VMEM((mats, slices // mats, voxels), jnp.bfloat16),
+            pltpu.VMEM((GROUPS, tiles, mats, rows, columns // GROUPS, pb), jnp.float32),
+            pltpu.VMEM((GROUPS, tiles, mats, rows, columns // GROUPS, pb), jnp.float32),
+            pltpu.VMEM((GROUPS, mats, rows, rays, pb), jnp.float32),
+            pltpu.VMEM((GROUPS, mats, rows, rays, pb), jnp.float32),
             pltpu.VMEM((GROUPS, rows, cbins, rays, pb), jnp.float32),
             pltpu.VMEM((GROUPS, cbins, rays, pb), jnp.float32),
             pltpu.VMEM((GROUPS, cbins, rays, pb), jnp.float32),
             dma((GROUPS,)),
+            dma((mats,)),
+            dma((mats,)),
             dma((GROUPS, tiles)),
             dma((GROUPS, tiles)),
             dma((GROUPS, mats)),
@@ -279,7 +319,7 @@
             collective_id=0, has_side_effects=True, vmem_limit_bytes=60 * 2**20
         ),
         name="project",
-    )(order, volume.reshape(slices, voxels), system.reshape(voxels, columns, pb), geometry, attenuation,
+    )(volume.reshape(mats, slices // mats, voxels), system.reshape(voxels, columns, pb), geometry, attenuation,
       response, crosstalk)
 
 

time: 32 us -> 29.9 us (0.934)
  Pallas kernels: 30 us -> 27.8 us
    pallas_call x1, Pallas kernels: 30 us -> 27.8 us  [per_device(): pl.pallas_call(functools.partial(kernel, mats, tiles, slices, voxels, vie...]
where the time goes in v2:
time: 29.9 us; the launch traced here: 29.7 us
  Pallas kernels  27.8 us (93%)
  local copies, waits for them, and re-layouts  1.88 us (6%)
    pallas_call x1, Pallas kernels, per_device(): pl.pallas_call(functools.partial(kernel, mats, tiles, slices, voxels, vie...  27.8 us
    unnamed x1, local copies, waits for them, and re-layouts  1.88 us

profile of v2, /device:TPU:1, one launch (start us, length us, event | category | flops | bytes accessed | tf_op | source)
XLA Modules:
  0.0 29.7 jit_solution(3012135887382015704)
XLA Ops:
  0.0 27.8 %project.1 = f32[8,2,16,512]{3,2,1,0:T(8,128)} custom-call(bf16[4,16,1024]{2,1,0:T(8,128)(2,1)} %bitcast.3, bf16[1024,32,128]{2,1,0:T(8,128)(2,1)} %bitcast.2, s32[8,16]{1,0:T(8,128)} %geometry_ref.1, f32[4,64]{1,0:T(4,128)} %attenuation_ref.1, f32[8,64]{1,0:T(8,128)} %response_ref.1, f32[8]{0:T(128)} %crosstalk_ref.1), custom_call_target="tpu_custom_call" | custom-call | tf_op jit(solution)/shard_map/project/pallas_call | solution.py:293
  27.8 1.9 %copy.8 = f32[8,2,16,512]{3,2,1,0:T(8,128)} copy(f32[8,2,16,512]{3,2,1,0:T(8,128)} %project.1) | data formatting | bytes 1048576

commit v3 on v2

--- a/solution.py
+++ b/solution.py
@@ -82,19 +82,34 @@
             send_sem=send0.at[peer], recv_sem=recv0.at[peer],
             device_id={"mat": peer}, device_id_type=MESH)
 
-    def copy1(g, off):
-        peer = lax.rem(me_tile + off, tiles)
-        return pltpu.make_async_remote_copy(
-            src_ref=partial_out.at[g, peer], dst_ref=partial_in.at[g, me_tile],
-            send_sem=send1.at[g, peer], recv_sem=recv1.at[g, me_tile],
+    known = {}
+
+    def partner(off):
+        if isinstance(off, int) and off in known:
+            return known[off]
+        peer, bit = 0, 1
+        while bit < tiles:
+            flip = (off // bit) % 2 if isinstance(off, int) else lax.rem(lax.div(off, bit), 2)
+            peer += lax.rem(lax.div(me_tile, bit) + flip, 2) * bit
+            bit *= 2
+        if isinstance(off, int):
+            known[off] = peer
+        return peer
+
+    def unit(ref, g, slot, part):
+        return ref.at[g, slot] if part is None else ref.at[g, slot, part]
+
+    def copy1(g, step, part, arrival=False):
+        peer = partner(tiles - step)
+        into = peer if arrival else me_tile
+        lane = g if part is None else g + part
+        return pltpu.make_async_remote_copy(
+            src_ref=unit(partial_out, g, peer, part), dst_ref=unit(partial_in, g, into, part),
+            send_sem=send1.at[lane, peer], recv_sem=recv1.at[lane, into],
             device_id={"tile": peer}, device_id_type=MESH)
 
-    def arrival1(g, off):
-        peer = lax.rem(me_tile + off, tiles)
-        return pltpu.make_async_remote_copy(
-            src_ref=partial_out.at[g, peer], dst_ref=partial_in.at[g, peer],
-            send_sem=send1.at[g, peer], recv_sem=recv1.at[g, peer],
-            device_id={"tile": peer}, device_id_type=MESH)
+    def parts(g):
+        return [None] if g < GROUPS - 1 else list(range(rows))
 
     def copy2(g, off):
         peer = lax.rem(me_mat + off, mats)
@@ -143,12 +158,15 @@
         by_row = jnp.swapaxes(jnp.stack(products, axis=0), 0, 1)
         by_row = by_row.reshape(mats, tiles, rows, group_cols, pb)
         for m in range(mats):
-            partial_out[g, :, m] = by_row[m]
-        loop(1, tiles, lambda off: copy1(g, off).start())
+            for r in range(rows):
+                partial_out[g, :, r, m] = by_row[m, :, r]
+        for part in parts(g):
+            loop(1, tiles, lambda step: copy1(g, step, part).start())
         partial_in[g, me_tile] = partial_out[g, me_tile]
 
-    def add_tiles(g):
-        loop(1, tiles, lambda off: arrival1(g, off).wait_recv())
+    def add_tiles(g, part=None):
+        loop(1, tiles, lambda step: copy1(g, step, part, arrival=True).wait_recv())
+        picks = list(range(rows)) if part is None else [part]
 
         sublane = lax.broadcasted_iota(jnp.int32, (group_cols, pb), 0)
         view = lax.rem(sublane, group_views)
@@ -163,15 +181,15 @@
             low_turned = jnp.logical_and(middle, jnp.logical_not(half))
             high_turned = jnp.logical_and(middle, half)
             for m in range(mats):
-                for r in range(rows):
-                    value = partial_in[g, tile, m, r]
+                for i, r in enumerate(picks):
+                    value = partial_in[g, tile, r, m]
                     turned = jnp.concatenate([value[group_views:], value[:group_views]], axis=0)
-                    at = 2 * (m * rows + r)
+                    at = 2 * (m * len(picks) + i)
                     sums[at] += jnp.where(low, value, jnp.where(low_turned, turned, 0.0))
                     sums[at + 1] += jnp.where(high, value, jnp.where(high_turned, turned, 0.0))
             return tuple(sums)
 
-        sums = tuple(jnp.zeros((group_cols, pb), jnp.float32) for _ in range(2 * mats * rows))
+        sums = tuple(jnp.zeros((group_cols, pb), jnp.float32) for _ in range(2 * mats * len(picks)))
         if tiles <= 8:
             for tile in range(tiles):
                 sums = add(tile, sums)
@@ -179,18 +197,22 @@
             sums = lax.fori_loop(0, tiles, add, sums)
         target = summed_out if g < EARLY else summed_in
         for m in range(mats):
-            for r in range(rows):
-                at = 2 * (m * rows + r)
+            for i, r in enumerate(picks):
+                at = 2 * (m * len(picks) + i)
                 target[g, m, r, :group_cols] = sums[at]
                 target[g, m, r, group_cols:] = sums[at + 1]
         if g < EARLY:
             loop(1, mats, lambda off: copy2(g, off).start())
             summed_in[g, me_mat] = summed_out[g, me_mat]
 
-    def detect(g):
+    def detect(g, part=None):
+        picks = list(range(rows)) if part is None else [part]
+        count_rows = len(picks) * rays
         if g < EARLY:
             loop(1, mats, lambda off: arrival2(g, off).wait_recv())
-        scaled = [summed_in[g, m].reshape(rows * rays, pb) * (-LOG2E) for m in range(mats)]
+        scaled = [
+            summed_in[g, m, picks[0]:picks[-1] + 1].reshape(count_rows, pb) * (-LOG2E) for m in range(mats)
+        ]
         unroll = 8
 
         def energies(block, totals):
@@ -205,19 +227,21 @@
                     totals[b] += response_ref[b, e] * passed
             return tuple(totals)
 
-        totals = tuple(jnp.zeros((rows * rays, pb), jnp.float32) for _ in range(cbins))
+        totals = tuple(jnp.zeros((count_rows, pb), jnp.float32) for _ in range(cbins))
         totals = lax.fori_loop(0, ebins // unroll, energies, totals)
         for b in range(cbins):
-            for r in range(rows):
-                detected[g, r, b] = totals[b][r * rays:(r + 1) * rays]
-
-        @pl.when(has_prev)
-        def _():
-            copy_down(g).start()
-
-        @pl.when(has_next)
-        def _():
-            copy_up(g).start()
+            for i, r in enumerate(picks):
+                detected[g, r, b] = totals[b][i * rays:(i + 1) * rays]
+
+        if 0 in picks:
+            @pl.when(has_prev)
+            def _():
+                copy_down(g).start()
+
+        if rows - 1 in picks:
+            @pl.when(has_next)
+            def _():
+                copy_up(g).start()
 
     def count(g):
         @pl.when(has_prev)
@@ -247,23 +271,26 @@
     def _():
         after[...] = jnp.zeros_like(after)
 
-    multiply(0)
-    multiply(1)
-    multiply(2)
-    add_tiles(0)
-    multiply(3)
-    add_tiles(1)
-    detect(0)
-    add_tiles(2)
-    detect(1)
-    add_tiles(3)
-    detect(2)
-    detect(3)
     for g in range(GROUPS):
+        multiply(g)
+    for g in range(EARLY):
+        add_tiles(g)
+    for g in range(EARLY):
+        detect(g)
+    for g in range(EARLY, GROUPS - 1):
+        add_tiles(g)
+        detect(g)
+    for g in range(EARLY):
+        count(g)
+    for part in parts(GROUPS - 1):
+        add_tiles(GROUPS - 1, part)
+        detect(GROUPS - 1, part)
+    for g in range(EARLY, GROUPS):
         count(g)
     loop(1, mats, lambda off: copy0(off).wait_send())
     for g in range(GROUPS):
-        loop(1, tiles, lambda off: copy1(g, off).wait_send())
+        for part in parts(g):
+            loop(1, tiles, lambda step: copy1(g, step, part).wait_send())
         if g < EARLY:
             loop(1, mats, lambda off: copy2(g, off).wait_send())
 
@@ -298,8 +325,8 @@
         scratch_shapes=[
             pltpu.VMEM((GROUPS, voxels, columns // GROUPS, pb), jnp.bfloat16),
             pltpu.VMEM((mats, slices // mats, voxels), jnp.bfloat16),
-            pltpu.VMEM((GROUPS, tiles, mats, rows, columns // GROUPS, pb), jnp.float32),
-            pltpu.VMEM((GROUPS, tiles, mats, rows, columns // GROUPS, pb), jnp.float32),
+            pltpu.VMEM((GROUPS, tiles, rows, mats, columns // GROUPS, pb), jnp.float32),
+            pltpu.VMEM((GROUPS, tiles, rows, mats, columns // GROUPS, pb), jnp.float32),
             pltpu.VMEM((GROUPS, mats, rows, rays, pb), jnp.float32),
             pltpu.VMEM((GROUPS, mats, rows, rays, pb), jnp.float32),
             pltpu.VMEM((GROUPS, rows, cbins, rays, pb), jnp.float32),
@@ -308,8 +335,8 @@
             dma((GROUPS,)),
             dma((mats,)),
             dma((mats,)),
-            dma((GROUPS, tiles)),
-            dma((GROUPS, tiles)),
+            dma((GROUPS + rows - 1, tiles)),
+            dma((GROUPS + rows - 1, tiles)),
             dma((GROUPS, mats)),
             dma((GROUPS, mats)),
             dma((GROUPS, 2)),

time: 29.9 us -> 32 us (1.070)
  the two profiles are of different devices: /device:TPU:1 before, /device:TPU:8 now
where the time goes in v3:
time: 32 us; the launch traced here: 31.8 us
  Pallas kernels  29.9 us (93%)
  local copies, waits for them, and re-layouts  1.88 us (6%)
    pallas_call x1, Pallas kernels, per_device(): pl.pallas_call(functools.partial(kernel, mats, tiles, slices, voxels, vie...  29.9 us
    unnamed x1, local copies, waits for them, and re-layouts  1.88 us

profile of v3, /device:TPU:8, one launch (start us, length us, event | category | flops | bytes accessed | tf_op | source)
XLA Modules:
  0.0 31.8 jit_solution(14399796179208367907)
XLA Ops:
  0.0 29.9 %project.1 = f32[8,2,16,512]{3,2,1,0:T(8,128)} custom-call(bf16[4,16,1024]{2,1,0:T(8,128)(2,1)} %bitcast.3, bf16[1024,32,128]{2,1,0:T(8,128)(2,1)} %bitcast.2, s32[8,16]{1,0:T(8,128)} %geometry_ref.1, f32[4,64]{1,0:T(4,128)} %attenuation_ref.1, f32[8,64]{1,0:T(8,128)} %response_ref.1, f32[8]{0:T(128)} %crosstalk_ref.1), custom_call_target="tpu_custom_call" | custom-call | tf_op jit(solution)/shard_map/project/pallas_call | solution.py:320
  29.9 1.9 %copy.8 = f32[8,2,16,512]{3,2,1,0:T(8,128)} copy(f32[8,2,16,512]{3,2,1,0:T(8,128)} %project.1) | data formatting | bytes 1048576

commit v4 on v3

--- a/solution.py
+++ b/solution.py
@@ -82,25 +82,11 @@
             send_sem=send0.at[peer], recv_sem=recv0.at[peer],
             device_id={"mat": peer}, device_id_type=MESH)
 
-    known = {}
-
-    def partner(off):
-        if isinstance(off, int) and off in known:
-            return known[off]
-        peer, bit = 0, 1
-        while bit < tiles:
-            flip = (off // bit) % 2 if isinstance(off, int) else lax.rem(lax.div(off, bit), 2)
-            peer += lax.rem(lax.div(me_tile, bit) + flip, 2) * bit
-            bit *= 2
-        if isinstance(off, int):
-            known[off] = peer
-        return peer
-
     def unit(ref, g, slot, part):
         return ref.at[g, slot] if part is None else ref.at[g, slot, part]
 
     def copy1(g, step, part, arrival=False):
-        peer = partner(tiles - step)
+        peer = lax.rem(me_tile + step, tiles)
         into = peer if arrival else me_tile
         lane = g if part is None else g + part
         return pltpu.make_async_remote_copy(

time: 32 us -> 31.4 us (0.981)
  the two profiles are of different devices: /device:TPU:8 before, /device:TPU:1 now
where the time goes in v4:
time: 31.4 us; the launch traced here: 31.2 us
  Pallas kernels  29.3 us (93%)
  local copies, waits for them, and re-layouts  1.88 us (6%)
    pallas_call x1, Pallas kernels, per_device(): pl.pallas_call(functools.partial(kernel, mats, tiles, slices, voxels, vie...  29.3 us
    unnamed x1, local copies, waits for them, and re-layouts  1.88 us

profile of v4, /device:TPU:1, one launch (start us, length us, event | category | flops | bytes accessed | tf_op | source)
XLA Modules:
  0.0 31.2 jit_solution(17442889563920959942)
XLA Ops:
  0.0 29.3 %project.1 = f32[8,2,16,512]{3,2,1,0:T(8,128)} custom-call(bf16[4,16,1024]{2,1,0:T(8,128)(2,1)} %bitcast.3, bf16[1024,32,128]{2,1,0:T(8,128)(2,1)} %bitcast.2, s32[8,16]{1,0:T(8,128)} %geometry_ref.1, f32[4,64]{1,0:T(4,128)} %attenuation_ref.1, f32[8,64]{1,0:T(8,128)} %response_ref.1, f32[8]{0:T(128)} %crosstalk_ref.1), custom_call_target="tpu_custom_call" | custom-call | tf_op jit(solution)/shard_map/project/pallas_call | solution.py:306
  29.4 1.9 %copy.8 = f32[8,2,16,512]{3,2,1,0:T(8,128)} copy(f32[8,2,16,512]{3,2,1,0:T(8,128)} %project.1) | data formatting | bytes 1048576
